TPU v7x, 256 devices: a whole 4x4x8 slice. The times are simulated.
256 devices in a mesh: tm: 8 (over x, core), row: 32 (over z, y).
Axes of the slice: x: 4, y: 4, z: 8, core: 2. Of those that a mesh axis runs over, the one named last changes fastest.
Arguments:
- image: float32 [8, 1, 2048, 2048], P('tm', None, 'row'), may hold values from -6 to 6
- relaxed: float32 [8, 1, 2048, 2048], P('tm', None, 'row'), may hold values from -6 to 6
- dual: float32 [8, 1, 2048, 2048], P('tm', None, 'row'), may hold values from -2 to 2
- sinogram: float32 [8, 12, 1, 2048], P('tm'), may hold values from -48 to 48
- angle_index: int32 [8, 12], P('tm'), may hold values from 0 to 31, as said below
- bin_offset: int32 [128, 32], P('row'), may hold values from 0 to 2047
- row_weight: float32 [32, 16], replicated, may hold values from 0.5 to 1.5
- response: bfloat16 [32, 128, 128], replicated, may hold values from -0.5 to 0.5
- row_gain: float32 [2048], P('row'), may hold values from 0.6 to 11.2
Outputs:
- image_new: float32 [8, 1, 2048, 2048], P('tm', None, 'row')
- dual_new: float32 [8, 1, 2048, 2048], P('tm', None, 'row')
Inputs may be any that keep to these rules, and one draw needn't show every extreme that they name: `angle_index`: the 12 views of one phase name distinct entries of the angle table.
All inputs are finite; a program needn't handle non-finite values.
Results may differ from a plain program's by a relative error of at most 0.0003.
Values sent between devices are 32-bit elements; how exact they have to be, the bound alone decides.
A program may use at most 64 MiB of HBM per device.

v0:
```python
import jax
import jax.numpy as jnp
from jax import lax
from jax.sharding import PartitionSpec as P

CG_ITERS = 3


HIGH = lax.Precision.HIGHEST
TAU_STEP = 0.1
SIGMA_STEP = 2.0
LAMBDA_BOUND = 2.0


def split_up(x, dim, devices):
    dims = x.shape
    blocks = x.reshape(*dims[:dim], devices, dims[dim] // devices, *dims[dim + 1 :])
    return jnp.moveaxis(blocks, dim, 0)


def sent_and_summed(x, axis, dim):
    blocks = split_up(x, dim, lax.axis_size(axis))
    arrived = lax.all_to_all(blocks, axis, split_axis=0, concat_axis=0, tiled=True)
    return arrived.sum(axis=0)


def filled_up(lines, devices):
    spare = -len(lines) % devices
    return jnp.pad(lines, [(0, spare)] + [(0, 0)] * (lines.ndim - 1))


def laid_out(blocks, dim):
    blocks = jnp.moveaxis(blocks, 0, dim)
    dims = blocks.shape
    return blocks.reshape(*dims[:dim], dims[dim] * dims[dim + 1], *dims[dim + 2 :])


def copy_for_each(x, axis):
    copies = jnp.broadcast_to(x, (lax.axis_size(axis), *x.shape))
    return lax.all_to_all(copies, axis, split_axis=0, concat_axis=0, tiled=True)


def gather_directly(x, axis, dim):
    return laid_out(copy_for_each(x, axis), dim)


def sum_by_parts(x, axes):
    own = sent_and_summed(filled_up(x, lax.axis_size(axes)), axes, 0)
    whole = gather_directly(own, axes, 0)
    return whole[: len(x)].reshape(x.shape)


def together(arrays, axis):
    ends = [0]
    for a in arrays:
        ends.append(ends[-1] + a.size)
    subtotal = sum_by_parts(jnp.concatenate([a.ravel() for a in arrays]), axis)
    return tuple((subtotal[b:e].reshape(a.shape) for a, b, e in zip(arrays, ends, ends[1:])))


def over_copies(x, axis):
    return copy_for_each(x, axis).sum(axis=0)


def with_halo(cells, sides, width):
    for axis, dim in sides:
        count = lax.axis_size(axis)
        head = lax.slice_in_dim(cells, 0, width, axis=dim)
        tail = lax.slice_in_dim(cells, cells.shape[dim] - width, cells.shape[dim], axis=dim)
        cells = jnp.concatenate(
            [
                lax.ppermute(tail, axis, [(i, (i + 1) % count) for i in range(count)]),
                cells,
                lax.ppermute(head, axis, [((i + 1) % count, i) for i in range(count)]),
            ],
            axis=dim,
        )
    return cells


def shifted(x, axis, by):
    devices = lax.axis_size(axis)
    return lax.ppermute(x, axis, [(i, (i + by) % devices) for i in range(devices)])


def view_tables(angles, row_weight, response, bin_offset):
    selector = angles[:, None] == jnp.arange(row_weight.shape[0], dtype=jnp.int32)[None, :]
    chosen = selector.astype(jnp.float32)
    weights = jnp.dot(chosen, row_weight, precision=HIGH)
    blocks = jnp.einsum("va,aio->vio", chosen, response.astype(jnp.float32), precision=HIGH)
    shifts = jnp.sum(jnp.where(selector[None, :, :], bin_offset[:, None, :], 0), axis=2)
    return (weights, blocks, shifts)


def shift_columns(rows, start):
    width = rows.shape[-1]
    doubled = jnp.concatenate([rows, rows], axis=-1)
    return lax.dynamic_slice_in_dim(doubled, start, width, axis=rows.ndim - 1)


def spread_view(rows, starts):
    width = rows.shape[-1]
    doubled = jnp.concatenate([rows, rows], axis=-1)

    def pick(start):
        return lax.dynamic_slice_in_dim(doubled, start, width, axis=rows.ndim - 1)

    return jax.vmap(pick)(starts)


def project(volume, weights, blocks, shifts):
    num_slices, num_rows, num_cols = volume.shape
    num_views, tile_rows = weights.shape
    block_width = blocks.shape[1]
    tile_count = num_rows // tile_rows
    tiled = volume.reshape(num_slices, tile_count, tile_rows, num_cols)
    summed = jnp.einsum("vj,skjc->vksc", weights, tiled, precision=HIGH)
    blocked = summed.reshape(
        num_views, tile_count, num_slices, num_cols // block_width, block_width
    )
    mapped = jnp.einsum("vksni,vio->vksno", blocked, blocks, precision=HIGH)
    mapped = mapped.reshape(num_views, tile_count, num_slices, num_cols)
    starts = (num_cols - jnp.transpose(shifts)) % num_cols
    rolled = jax.vmap(jax.vmap(shift_columns))(mapped, starts)
    return jnp.sum(rolled, axis=1)


def backproject(projected, weights, blocks, shifts):
    num_views, num_slices, num_cols = projected.shape
    tile_rows = weights.shape[1]
    block_width = blocks.shape[1]
    tile_count = shifts.shape[0]
    starts = jnp.transpose(shifts) % num_cols
    picked = jax.vmap(spread_view)(projected, starts)
    blocked = picked.reshape(
        num_views, tile_count, num_slices, num_cols // block_width, block_width
    )
    mapped = jnp.einsum("vksno,vio->vksni", blocked, blocks, precision=HIGH)
    mapped = mapped.reshape(num_views, tile_count, num_slices, num_cols)
    tiled = jnp.einsum("vj,vksc->skjc", weights, mapped, precision=HIGH)
    return tiled.reshape(num_slices, tile_count * tile_rows, num_cols)


def measure(volume, tables, gain):
    partial_value = project(volume * gain, tables[0], tables[1], tables[2])
    total, squared = together((partial_value, jnp.sum(volume * volume)), "row")
    return (total, squared)


def squares(resid):
    return over_copies(jnp.sum(resid * resid), "row")


def local(image, relaxed, dual, sinogram, angle_index, bin_offset, row_weight, response, row_gain):
    padded = with_halo(relaxed, (("tm", 0),), 1)
    earlier = shifted(dual, "tm", 1)
    dual_new = jnp.clip(dual + SIGMA_STEP * (padded[2:] - relaxed), -LAMBDA_BOUND, LAMBDA_BOUND)
    behind = jnp.clip(earlier + SIGMA_STEP * (relaxed - padded[:1]), -LAMBDA_BOUND, LAMBDA_BOUND)
    primal = image - TAU_STEP * (behind - dual_new)
    gain = row_gain[None, :, None]
    tables = view_tables(angle_index[0], row_weight, response, bin_offset)
    solution = primal[0]
    start_proj, unused = measure(solution, tables, gain)
    resid = backproject(sinogram[0] - start_proj, tables[0], tables[1], tables[2]) * gain
    direction = resid
    norm_now = squares(resid)
    for step in range(CG_ITERS):
        total, squared = measure(direction, tables, gain)
        image_w = backproject(total, tables[0], tables[1], tables[2]) * gain + direction / TAU_STEP
        product = jnp.sum(total * total) + squared / TAU_STEP
        alpha = norm_now / product
        solution = solution + alpha * direction
        resid = resid - alpha * image_w
        if step + 1 < CG_ITERS:
            norm_next = squares(resid)
            direction = resid + norm_next / norm_now * direction
            norm_now = norm_next
    return (solution[None], dual_new)


def solution(mesh):
    return jax.shard_map(
        local,
        mesh=mesh,
        in_specs=(
            P("tm", None, "row", None),
            P("tm", None, "row", None),
            P("tm", None, "row", None),
            P("tm", None, None, None),
            P("tm", None),
            P("row", None),
            P(),
            P(),
            P("row"),
        ),
        out_specs=(P("tm", None, "row", None), P("tm", None, "row", None)),
        check_vma=False,
    )
```

profile of v0, /device:TPU:2, one launch (start us, length us, event | category | flops | bytes accessed | tf_op | source)
XLA Modules:
  0.0 1146.5 jit_solution(13010842301999445435)
XLA Ops:
  6.0 9.2 collective-permute-done
  21.6 125.1 %while.7 = (s32[]{:T(128)}, f32[12,4,1,4096]{3,2,1,0:T(1,128)S(1)}, s32[48,4]{0,1:T(4,128)S(1)}, f32[48,1,2048]{2,1,0:T(1,128)S(1)}, s32[]{:T(128)}) while((s32[]{:T(128)}, f32[12,4,1,4096]{3,2,1,0:T(1,128)S(1)}, s32[48,4]{0,1:T(4,128)S(1)}, f32[48,1,2048]{2,1,0:T(1,128)S(1)}, s32[]{:T(128)}) %tuple.121), condition=%wide.while_cond, body=%wide.while_body.sunk | while | flops 2 | bytes 16529 | solution.py:98
  149.0 21.7 %all_to_all.80 = f32[32,1,769]{2,1,0:T(1,128)S(1)} all-to-all(f32[32,1,769]{2,1,0:T(1,128)S(1)} %all_to_all.52), channel_id=1, replica_groups=mesh['tm'=8,'row'=32] {'row'}, dimensions={0} | all-to-all | bytes 196864 | tf_op jit(solution)/shard_map/all_to_all | solution.py:23
  171.5 4.0 all-to-all-start.1
  175.8 10.1 all-to-all-done.1
  187.8 91.6 %while.8 = (s32[]{:T(128)}, f32[12,1,4096]{2,1,0:T(1,128)S(1)}, s32[48,3]{0,1:T(4,128)S(1)}, f32[48,1,2048]{2,1,0:T(1,128)S(1)}, s32[]{:T(128)}) while((s32[]{:T(128)}, f32[12,1,4096]{2,1,0:T(1,128)S(1)}, s32[48,3]{0,1:T(4,128)S(1)}, f32[48,1,2048]{2,1,0:T(1,128)S(1)}, s32[]{:T(128)}) %tuple.124), condition=%wide.while_cond.1, body=%wide.while_body.1.sunk | while | flops 2 | bytes 16509 | solution.py:106
  286.6 162.4 %while.9 = (s32[]{:T(128)}, f32[12,4,1,4096]{3,2,1,0:T(1,128)}, s32[48,4]{0,1:T(4,128)S(1)}, f32[48,1,2048]{2,1,0:T(1,128)S(1)}, s32[]{:T(128)}) while((s32[]{:T(128)}, f32[12,4,1,4096]{3,2,1,0:T(1,128)}, s32[48,4]{0,1:T(4,128)S(1)}, f32[48,1,2048]{2,1,0:T(1,128)S(1)}, s32[]{:T(128)}) %tuple.142), condition=%wide.while_cond.2, body=%wide.while_body.2.sunk | while | flops 2 | bytes 16529 | solution.py:98
  287.3 2.7 bitcast_dynamic-update-slice_fusion.9
  290.7 2.7 bitcast_dynamic-update-slice_fusion.9
  294.0 2.7 bitcast_dynamic-update-slice_fusion.9
  297.4 2.7 bitcast_dynamic-update-slice_fusion.9
  300.8 2.7 bitcast_dynamic-update-slice_fusion.9
  304.2 2.7 bitcast_dynamic-update-slice_fusion.9
  307.6 2.7 bitcast_dynamic-update-slice_fusion.9
  311.0 2.7 bitcast_dynamic-update-slice_fusion.9
  314.3 2.7 bitcast_dynamic-update-slice_fusion.9
  317.7 2.7 bitcast_dynamic-update-slice_fusion.9
  321.1 2.7 bitcast_dynamic-update-slice_fusion.9
  324.5 2.7 bitcast_dynamic-update-slice_fusion.9
  327.9 2.7 bitcast_dynamic-update-slice_fusion.9
  331.3 2.7 bitcast_dynamic-update-slice_fusion.9
  334.6 2.7 bitcast_dynamic-update-slice_fusion.9
  338.0 2.7 bitcast_dynamic-update-slice_fusion.9
  351.6 2.7 bitcast_dynamic-update-slice_fusion.9
  365.1 2.7 bitcast_dynamic-update-slice_fusion.9
  382.0 2.7 bitcast_dynamic-update-slice_fusion.9
  398.9 2.7 bitcast_dynamic-update-slice_fusion.9
  415.9 2.7 bitcast_dynamic-update-slice_fusion.9
  429.4 2.7 bitcast_dynamic-update-slice_fusion.9
  446.3 2.7 bitcast_dynamic-update-slice_fusion.9
  451.2 13.5 %all_to_all.78 = f32[32,1,769]{2,1,0:T(1,128)S(1)} all-to-all(f32[32,1,769]{2,1,0:T(1,128)S(1)} %all_to_all.56), channel_id=1, replica_groups=mesh['tm'=8,'row'=32] {'row'}, dimensions={0} | all-to-all | bytes 196864 | tf_op jit(solution)/shard_map/all_to_all | solution.py:23
  465.9 3.8 all-to-all-start.2
  469.8 9.6 all-to-all-done.2
  480.1 4.1 all-to-all-start.4
  484.9 9.7 all-to-all-done.4
  496.6 101.6 %while.10 = (s32[]{:T(128)}, f32[12,1,4096]{2,1,0:T(1,128)S(1)}, s32[48,3]{0,1:T(4,128)S(1)}, f32[48,1,2048]{2,1,0:T(1,128)S(1)}, s32[]{:T(128)}) while((s32[]{:T(128)}, f32[12,1,4096]{2,1,0:T(1,128)S(1)}, s32[48,3]{0,1:T(4,128)S(1)}, f32[48,1,2048]{2,1,0:T(1,128)S(1)}, s32[]{:T(128)}) %tuple.145), condition=%wide.while_cond.3, body=%wide.while_body.3.sunk | while | flops 2 | bytes 16509 | solution.py:106
  605.5 3.8 all-to-all-start.5
  609.4 9.8 all-to-all-done.5
  628.6 159.3 %while.11 = (s32[]{:T(128)}, f32[12,4,1,4096]{3,2,1,0:T(1,128)}, s32[48,4]{0,1:T(4,128)S(1)}, f32[48,1,2048]{2,1,0:T(1,128)S(1)}, s32[]{:T(128)}) while((s32[]{:T(128)}, f32[12,4,1,4096]{3,2,1,0:T(1,128)}, s32[48,4]{0,1:T(4,128)S(1)}, f32[48,1,2048]{2,1,0:T(1,128)S(1)}, s32[]{:T(128)}) %tuple.143), condition=%wide.while_cond.4, body=%wide.while_body.4.sunk | while | flops 2 | bytes 16529 | solution.py:98
  793.4 13.4 %all_to_all.81 = f32[32,1,769]{2,1,0:T(1,128)S(1)} all-to-all(f32[32,1,769]{2,1,0:T(1,128)S(1)} %all_to_all.60), channel_id=1, replica_groups=mesh['tm'=8,'row'=32] {'row'}, dimensions={0} | all-to-all | bytes 196864 | tf_op jit(solution)/shard_map/all_to_all | solution.py:23
  807.5 4.1 all-to-all-start.7
  811.7 10.4 all-to-all-done.7
  826.6 126.8 %while.12 = (s32[]{:T(128)}, f32[12,1,4096]{2,1,0:T(1,128)}, s32[48,3]{0,1:T(4,128)S(1)}, f32[48,1,2048]{2,1,0:T(1,128)S(1)}, s32[]{:T(128)}) while((s32[]{:T(128)}, f32[12,1,4096]{2,1,0:T(1,128)}, s32[48,3]{0,1:T(4,128)S(1)}, f32[48,1,2048]{2,1,0:T(1,128)S(1)}, s32[]{:T(128)}) %tuple.146), condition=%wide.while_cond.5, body=%wide.while_body.5.sunk | while | flops 2 | bytes 16509 | solution.py:106
  957.0 3.7 multiply_reduce_fusion.1
  961.2 12.9 %all_to_all.82 = f32[32,1,1]{2,1,0:T(1,128)S(1)} all-to-all(f32[32,1,1]{2,1,0:T(1,128)S(1)} %broadcast_in_dim.67), channel_id=1, replica_groups=mesh['tm'=8,'row'=32] {'row'}, dimensions={0} | all-to-all | bytes 256 | tf_op jit(solution)/shard_map/all_to_all | solution.py:40
  982.8 127.4 %while.13 = (s32[]{:T(128)}, f32[12,4,1,4096]{3,2,1,0:T(1,128)S(1)}, s32[48,4]{0,1:T(4,128)S(1)}, f32[48,1,2048]{2,1,0:T(1,128)S(1)}, s32[]{:T(128)}) while((s32[]{:T(128)}, f32[12,4,1,4096]{3,2,1,0:T(1,128)S(1)}, s32[48,4]{0,1:T(4,128)S(1)}, f32[48,1,2048]{2,1,0:T(1,128)S(1)}, s32[]{:T(128)}) %tuple.144), condition=%wide.while_cond.6, body=%wide.while_body.6.sunk | while | flops 2 | bytes 16529 | solution.py:98
  1112.5 14.3 %all_to_all.83 = f32[32,1,769]{2,1,0:T(1,128)S(1)} all-to-all(f32[32,1,769]{2,1,0:T(1,128)S(1)} %all_to_all.64), channel_id=1, replica_groups=mesh['tm'=8,'row'=32] {'row'}, dimensions={0} | all-to-all | bytes 196864 | tf_op jit(solution)/shard_map/all_to_all | solution.py:23
  1127.0 13.6 %all_to_all.79 = f32[32,1,769]{2,1,0:T(1,128)S(1)} all-to-all(f32[32,1,769]{2,1,0:T(1,128)S(1)} %broadcast_in_dim.68), channel_id=1, replica_groups=mesh['tm'=8,'row'=32] {'row'}, dimensions={0} | all-to-all | bytes 196864 | tf_op jit(solution)/shard_map/all_to_all | solution.py:40
  (1133 shorter events, 897.2 us)
Async XLA Ops:
  0.6 4.7 copy-start
  0.6 14.6 %collective-permute-start.1 = (f32[1,1,64,2048]{3,2,1,0:T(8,128)}, f32[1,1,64,2048]{3,2,1,0:T(8,128)S(1)}, u32[]{:S(2)}, u32[]{:S(2)}) collective-permute-start(f32[1,1,64,2048]{3,2,1,0:T(8,128)} %param.10), channel_id=1, source_target_pairs={{0,32},{32,64},{64,96},{96,128},{128,160},{160,192},{192,224},{224... | collective-permute-start | bytes 1572872 | tf_op jit(solution)/shard_map/ppermute | solution.py:72
  0.7 14.5 %collective-permute-start.2 = (f32[1,1,64,2048]{3,2,1,0:T(8,128)}, f32[1,1,64,2048]{3,2,1,0:T(8,128)S(1)}, u32[]{:S(2)}, u32[]{:S(2)}) collective-permute-start(f32[1,1,64,2048]{3,2,1,0:T(8,128)} %param.10), channel_id=1, source_target_pairs={{32,0},{64,32},{96,64},{128,96},{160,128},{192,160},{224,192},{0,2... | collective-permute-start | bytes 1572872 | tf_op jit(solution)/shard_map/ppermute | solution.py:74
  2.4 12.8 %collective-permute-start = (f32[1,1,64,2048]{3,2,1,0:T(8,128)}, f32[1,1,64,2048]{3,2,1,0:T(8,128)}, u32[]{:S(2)}, u32[]{:S(2)}) collective-permute-start(f32[1,1,64,2048]{3,2,1,0:T(8,128)} %param.11), channel_id=1, source_target_pairs={{0,32},{32,64},{64,96},{96,128},{128,160},{160,192},{192,224},{224... | collective-permute-start | bytes 1572872 | tf_op jit(solution)/shard_map/ppermute | solution.py:83
  3.1 279.6 %copy-start.9 = (f32[4,16]{1,0:T(4,128)}, f32[4,16]{1,0:T(4,128)S(1)}, u32[]{:S(2)}) copy-start(f32[4,16]{1,0:T(4,128)S(1)} %mul.371) | copy-start | bytes 772
  3.1 0.7 copy-start.13
  3.1 0.7 copy-start.14
  4.4 0.7 copy-start.16
  5.3 9.9 copy-start.6
  5.3 9.9 copy-start.7
  5.3 9.9 copy-start.8
  17.9 0.8 copy-start.3
  171.5 14.5 %all-to-all-start.1 = ((f32[32,1,769]{2,1,0:T(1,128)}), f32[32,1,769]{2,1,0:T(1,128)S(1)}, u32[]{:S(2)}, u32[]{:S(2)}) async-start(f32[32,1,769]{2,1,0:T(1,128)} %broadcast_in_dim.61), calls=%async_computation.1 | async-start | bytes 229376 | tf_op jit(solution)/shard_map/all_to_all | solution.py:40
  186.4 0.9 copy-start.12
  465.9 13.5 %all-to-all-start.2 = ((f32[32,1,1]{2,1,0:T(1,128)}), f32[32,1,1]{2,1,0:T(1,128)S(1)}, u32[]{:S(2)}, u32[]{:S(2)}) async-start(f32[32,1,1]{2,1,0:T(1,128)} %broadcast_in_dim.63), calls=%async_computation.2 | async-start | bytes 32768 | tf_op jit(solution)/shard_map/all_to_all | solution.py:40
  480.1 14.5 %all-to-all-start.4 = ((f32[32,1,769]{2,1,0:T(1,128)}), f32[32,1,769]{2,1,0:T(1,128)S(1)}, u32[]{:S(2)}, u32[]{:S(2)}) async-start(f32[32,1,769]{2,1,0:T(1,128)} %broadcast_in_dim.64), calls=%async_computation.4 | async-start | bytes 229376 | tf_op jit(solution)/shard_map/all_to_all | solution.py:40
  600.7 1.3 copy-start.10
  605.5 13.6 %all-to-all-start.5 = ((f32[32,1,1]{2,1,0:T(1,128)}), f32[32,1,1]{2,1,0:T(1,128)S(1)}, u32[]{:S(2)}, u32[]{:S(2)}) async-start(f32[32,1,1]{2,1,0:T(1,128)} %broadcast_in_dim.65), calls=%async_computation.5 | async-start | bytes 32768 | tf_op jit(solution)/shard_map/all_to_all | solution.py:40
  807.5 14.5 %all-to-all-start.7 = ((f32[32,1,769]{2,1,0:T(1,128)}), f32[32,1,769]{2,1,0:T(1,128)S(1)}, u32[]{:S(2)}, u32[]{:S(2)}) async-start(f32[32,1,769]{2,1,0:T(1,128)} %broadcast_in_dim.66), calls=%async_computation.7 | async-start | bytes 229376 | tf_op jit(solution)/shard_map/all_to_all | solution.py:40
  955.8 1.1 copy-start.11
  976.0 1.9 copy-start.2
  1111.5 32.6 %copy-start.5 = (f32[4,2048,16]{1,2,0:T(8,128)S(1)}, f32[4,2048,16]{1,2,0:T(8,128)}, u32[]{:S(2)}) copy-start(f32[4,2048,16]{1,2,0:T(8,128)} %get-tuple-element.149) | copy-start | bytes 1572868
  1112.5 31.7 %copy-start.4 = (f32[1,1,64,2048]{3,2,1,0:T(8,128)S(1)}, f32[1,1,64,2048]{3,2,1,0:T(8,128)}, u32[]{:S(2)}) copy-start(f32[1,1,64,2048]{3,2,1,0:T(8,128)} %copy-done.3) | copy-start | bytes 1572868
  1126.8 17.4 %copy-start.1 = (f32[4,2048,16]{1,2,0:T(8,128)S(1)}, f32[4,2048,16]{1,2,0:T(8,128)}, u32[]{:S(2)}) copy-start(f32[4,2048,16]{1,2,0:T(8,128)} %get-tuple-element.148) | copy-start | bytes 1572868
  1144.1 0.7 copy-start.15
where the time goes:
time: 1170 us; the launch traced here: 1150 us
  local copies, waits for them, and re-layouts  910 us (78%)
  blocking collectives  89.4 us (8%)
  waiting for transfers between devices  58.8 us (5%)
  other arithmetic  29 us (2%)
  matrix products  22.6 us (2%)
  starting transfers between devices  21.6 us (2%)
    gather x1008, local copies, waits for them, and re-layouts  889 us
    all_to_all x4, blocking collectives, sent_and_summed(): lax.all_to_all(blocks, axis, split_axis=0, concat_axis=0, tiled=True)  62.9 us
    all_to_all x5, waiting for transfers between devices, copy_for_each(): return lax.all_to_all(copies, axis, split_axis=0, concat_axis=0, tiled=True)  49.6 us
    all_to_all x2, blocking collectives, copy_for_each(): return lax.all_to_all(copies, axis, split_axis=0, concat_axis=0, tiled=True)  26.5 us
  transfers between devices with their start and end apart: 8, of which 6 were waited for; matrix products, arithmetic and copies ran while one was open for 0% of the time, Pallas kernels for 0%

commit v1 on v0

v1 whole, which is shorter than its diff:
```python
import jax
import jax.numpy as jnp
from jax import lax
from jax.experimental import pallas as pl
from jax.experimental.pallas import tpu as pltpu
from jax.sharding import PartitionSpec as P

MESH = pl.DeviceIdType.MESH
F32 = jnp.float32
BF16 = jnp.bfloat16

CG_ITERS = 3
TAU_STEP = 0.1
SIGMA_STEP = 2.0
LAMBDA_BOUND = 2.0

COLS = 2048
BLK = 128
NB = COLS // BLK
TR = 16
VIEWS = 12
VPAD = 16
HALVES = 2 * VIEWS
NZ, NY = 8, 4
NR = NZ * NY
GROUP = 2 * NY
GROUP_ROWS = NR // GROUP
CHUNKS = HALVES // GROUP
PAIRS = 80
ROUNDS = NZ // 2 + NY // 2 - 1
VMEM_LIMIT = 60 * 1024 * 1024

OTHERS = sorted(
    ((dz, dy) for dz in range(NZ) for dy in range(NY) if dz or dy),
    key=lambda d: -(min(d[0], NZ - d[0]) + min(d[1], NY - d[1])),
)
MEMBERS = sorted(
    ((dz, dy) for dz in range(2) for dy in range(NY) if dz or dy),
    key=lambda d: -(d[0] + min(d[1], NY - d[1])),
)


def split(x):
    hi = x.astype(BF16)
    lo = (x - hi.astype(F32)).astype(BF16)
    return hi, lo


def small_dot(a, b):
    ah, al = split(a)
    bh, bl = split(b)
    return jnp.dot(
        jnp.concatenate([ah, ah, al], axis=1),
        jnp.concatenate([bh, bl, bh], axis=0),
        preferred_element_type=F32,
    )


def solve_kernel(
    angles, offsets,
    image, relaxed, dual, sinogram, row_weight, response, gain, offsets_v,
    x0_out, step_out, next_out,
    img, rel, dua, rel_next, s_own, s_prev, resp, sino,
    table, wts, pairs, dg, rf, rt, dbl, lhs, mapped, mix, ys,
    part, total, got, got_group, rho, pi, gpi, xi,
    off_own, off_all, gain_own, gain_all, off_group, far_in, turn,
    load_sem, misc_sem, round_sem, rel_send, rel_recv, s_send, s_recv,
    tab_send, tab_recv, rs_send, rs_recv, ag_send, ag_recv, grs_send, grs_recv, gag_send, gag_recv, *tmp,
):
    nt = lax.axis_size("tm")
    t, me = lax.axis_index("tm"), lax.axis_index("row")
    after, before = lax.rem(t + 1, nt), lax.rem(t + nt - 1, nt)
    z, y = me // NY, lax.rem(me, NY)
    low = lax.rem(z, 2)
    place_in_group = low * NY + y
    tiles = img.shape[0]
    group_tiles = tiles * NR // GROUP
    lane = lax.broadcasted_iota(jnp.int32, (NB, BLK), 1)

    def there(dz, dy):
        return lax.rem(z + dz, NZ) * NY + lax.rem(y + dy, NY)

    def source(dz, dy):
        return there(NZ - dz, NY - dy)

    def load(i, k):
        src, dst = ((relaxed, rel), (dual, dua), (image, img))[i]
        return pltpu.make_async_copy(src.at[pl.ds(k * TR, TR), :], dst.at[k], load_sem.at[i, k])

    for k in range(tiles):
        load(0, k).start()
        load(1, k).start()

    near = [there(1, 0), there(NZ - 1, 0), there(0, 1), there(0, NY - 1)]
    barrier = pltpu.get_barrier_semaphore()
    for other in (after, before):
        pl.semaphore_signal(barrier, inc=1, device_id=(other, me), device_id_type=MESH)
    for other in near:
        pl.semaphore_signal(barrier, inc=1, device_id=(t, other), device_id_type=MESH)
    fetch_resp = pltpu.make_async_copy(response, resp, misc_sem.at[0])
    fetch_resp.start()
    for k in range(tiles):
        load(2, k).start()
    fetch_sino = pltpu.make_async_copy(sinogram, sino, misc_sem.at[1])
    fetch_sino.start()
    pl.semaphore_wait(barrier, len(near) + 2)

    rel_copies = [
        pltpu.make_async_remote_copy(
            rel.at[k], rel_next.at[k], rel_send.at[k], rel_recv.at[k],
            device_id=(before, me), device_id_type=MESH,
        )
        for k in range(tiles)
    ]
    s_copies = [
        pltpu.make_async_remote_copy(
            s_own.at[k], s_prev.at[k], s_send.at[k], s_recv.at[k],
            device_id=(after, me), device_id_type=MESH,
        )
        for k in range(tiles)
    ]
    for k in range(tiles):
        load(0, k).wait()
        rel_copies[k].start()
        load(1, k).wait()
        s_own[k] = dua[k] - SIGMA_STEP * rel[k]
        if k > 0:
            s_copies[k - 1].start()
    off_own[0:tiles, 0 : offsets_v.shape[1]] = offsets_v[...]
    gain_own[0:1, 0 : gain.shape[1]] = gain[...]
    s_copies[tiles - 1].start()

    for i in range(ROUNDS):
        for other in near:
            pl.semaphore_signal(round_sem.at[i], inc=1, device_id=(t, other), device_id_type=MESH)
        if i == 0:
            fetch_resp.wait()
            wts[...] = jnp.zeros_like(wts)
            table[...] = jnp.transpose(row_weight[...])
            for v in range(VIEWS):
                a = angles[0, v]
                wts[v : v + 1, :] = table[pl.ds(a, 1), :]
                r = resp[a]
                rf[v, 0:BLK, :] = r
                rf[v, BLK : 2 * BLK, :] = r
                flipped = jnp.transpose(r.astype(F32)).astype(BF16)
                rt[v, 0:BLK, :] = flipped
                rt[v, BLK : 2 * BLK, :] = flipped
            for k in range(tiles):
                dg[k] = wts[...] * gain[:, k * TR : (k + 1) * TR]
            ys[...] = jnp.zeros_like(ys)
            pairs[...] = jnp.zeros_like(pairs)
            row = 0
            for v in range(VIEWS):
                pairs[row : row + VIEWS - v, :] = wts[v : v + 1, :] * wts[v:VIEWS, :]
                row += VIEWS - v
        pl.semaphore_wait(round_sem.at[i], len(near))

    share = GROUP_ROWS
    taker, slot_there = me // share, lax.rem(me, share)

    def tables(g):
        other = g * GROUP + taker
        return [
            pltpu.make_async_remote_copy(
                own, every.at[slot_there], tab_send.at[i, g], tab_recv.at[i, slot_there],
                device_id=(t, other), device_id_type=MESH,
            )
            for i, (own, every) in enumerate(((off_own, off_all), (gain_own, gain_all)))
        ]

    for g in range(NR // GROUP):
        @pl.when(g * GROUP + taker != me)
        def _(g=g):
            for c in tables(g):
                c.start()

    def arrived(i, j):
        own, every = ((off_own, off_all), (gain_own, gain_all))[i]
        return pltpu.make_async_remote_copy(
            own, every.at[j], tab_send.at[i, 0], tab_recv.at[i, j],
            device_id=(t, me), device_id_type=MESH,
        )

    def group_tables():
        for j in range(share):
            @pl.when(place_in_group * share + j != me)
            def _(j=j):
                arrived(0, j).wait_recv()
                arrived(1, j).wait_recv()

            @pl.when(place_in_group * share + j == me)
            def _(j=j):
                off_all[j] = off_own[...]
                gain_all[j] = gain_own[...]
        to_smem = pltpu.make_async_copy(off_all, off_group, misc_sem.at[2])
        to_smem.start()
        ph, plo = split(pairs[...])
        stacked = jnp.concatenate([ph, ph, plo], axis=1)
        for j in range(share):
            column = jnp.transpose(gain_all[j])[0 : tiles * TR, 0:1]
            squares = jnp.broadcast_to(column * column, (tiles * TR, BLK))
            for k in range(tiles):
                gh, gl = split(squares[k * TR : (k + 1) * TR])
                mix[j * tiles + k] = jnp.dot(
                    stacked, jnp.concatenate([gh, gl, gh], axis=0), preferred_element_type=F32
                )
        for g in range(NR // GROUP):
            @pl.when(g * GROUP + taker != me)
            def _(g=g):
                for c in tables(g):
                    c.wait_send()
        to_smem.wait()
        for k in range(group_tiles):
            for v in range(VIEWS):
                off = off_group[k // tiles, k % tiles, angles[0, v]]
                far_in[k * VIEWS + v] = lax.shift_right_logical(off, 7)
                turn[k * VIEWS + v] = off & (BLK - 1)

    def own_shift(k, v):
        off = offsets[k, angles[0, v]]
        return lax.shift_right_logical(off, 7), off & (BLK - 1)

    def group_shift(k, v):
        return far_in[k * VIEWS + v], turn[k * VIEWS + v]

    def roll_out(count, shift):
        for v in range(VIEWS):
            mapped[v, 0 : count * NB, :] = jnp.dot(
                lhs[v, 0 : count * NB, :], rf[v], preferred_element_type=F32
            )
        for v in range(VIEWS):
            twice = tmp[v]
            for k in range(count):
                turned = pltpu.roll(mapped[v, k * NB : (k + 1) * NB, :], shift(k, v)[1], 1)
                twice[k, 0:NB, :] = turned
                twice[k, NB : 2 * NB, :] = turned
            acc = None
            for k in range(count):
                q, r = shift(k, v)
                near_rows = twice[k, pl.ds(NB - q, NB), :]
                far_rows = twice[k, pl.ds(NB - 1 - q, NB), :]
                one = jnp.where(lane >= r, near_rows, far_rows)
                acc = one if acc is None else acc + one
            part[2 * v] = acc[0:8]
            part[2 * v + 1] = acc[8:16]

    def roll_back(w, count, shift):
        dbl[:, 0:NB, :] = w
        dbl[:, NB : 2 * NB, :] = w
        for v in range(VIEWS):
            for k in range(count):
                q, r = shift(k, v)
                near_rows = dbl[v, pl.ds(q, NB), :]
                far_rows = dbl[v, pl.ds(q + 1, NB), :]
                e = pltpu.roll(jnp.where(lane >= r, near_rows, far_rows), (BLK - r) & (BLK - 1), 1)
                hi, lo = split(e)
                lhs[v, k * NB : (k + 1) * NB, 0:BLK] = hi
                lhs[v, k * NB : (k + 1) * NB, BLK : 2 * BLK] = lo

    def scatter(i):
        other = there(*OTHERS[i])
        return pltpu.make_async_remote_copy(
            part.at[other], got.at[i], rs_send, rs_recv, device_id=(t, other), device_id_type=MESH
        )

    def gather(i):
        return pltpu.make_async_remote_copy(
            total.at[me], total.at[me], ag_send, ag_recv,
            device_id=(t, there(*OTHERS[i])), device_id_type=MESH,
        )

    def wait_for(chunks, sem):
        pltpu.make_async_copy(got.at[pl.ds(0, chunks)], got.at[pl.ds(0, chunks)], sem).wait()

    def sum_rows(meanwhile):
        for i in range(len(OTHERS)):
            @pl.when(there(*OTHERS[i]) < HALVES)
            def _(i=i):
                scatter(i).start()

        meanwhile()

        @pl.when(me < HALVES)
        def _():
            wait_for(NR - 1, rs_recv)
            acc = part[me]
            for i in range(len(OTHERS)):
                acc = acc + got[i]
            total[me] = acc
            for i in range(len(OTHERS)):
                gather(i).start()
            wait_for(HALVES - 1, rs_send)
            wait_for(HALVES - 1, ag_recv)
            wait_for(NR - 1, ag_send)

        @pl.when(me >= HALVES)
        def _():
            wait_for(HALVES, rs_send)
            wait_for(HALVES, ag_recv)

    def place(dz, dy):
        return lax.rem(low + dz, 2) * NY + lax.rem(y + dy, NY)

    def member(dz, dy):
        return (z - low) * NY + place(dz, dy)

    def group_scatter(dz, dy):
        i = dz * NY + dy
        return pltpu.make_async_remote_copy(
            part.at[pl.ds(place(dz, dy) * CHUNKS, CHUNKS)], got_group.at[i], grs_send.at[i], grs_recv.at[i],
            device_id=(t, member(dz, dy)), device_id_type=MESH,
        )

    def group_gather(dz, dy, owner):
        i = dz * NY + dy
        chunk = pl.ds(owner * CHUNKS, CHUNKS)
        return pltpu.make_async_remote_copy(
            total.at[chunk], total.at[chunk], gag_send.at[i], gag_recv.at[i],
            device_id=(t, member(dz, dy)), device_id_type=MESH,
        )

    def sum_group():
        for d in MEMBERS:
            group_scatter(*d).start()
        mine = pl.ds(place_in_group * CHUNKS, CHUNKS)
        acc = part[mine]
        for d in reversed(MEMBERS):
            group_scatter(*d).wait_recv()
            acc = acc + got_group[d[0] * NY + d[1]]
        total[mine] = acc
        for d in MEMBERS:
            group_gather(*d, place_in_group).start()
        for d in MEMBERS:
            group_scatter(*d).wait_send()
        for d in reversed(MEMBERS):
            group_gather(*d, place(2 - d[0], NY - d[1])).wait_recv()
        for d in MEMBERS:
            group_gather(*d, place_in_group).wait_send()

    def summed():
        return total[...].reshape(VIEWS, NB, BLK)

    for k in range(tiles):
        rows = pl.ds(k * TR, TR)
        s_copies[k].wait_recv()
        rel_copies[k].wait_recv()
        load(2, k).wait()
        behind = jnp.clip(s_prev[k] + SIGMA_STEP * rel[k], -LAMBDA_BOUND, LAMBDA_BOUND)
        ahead = jnp.clip(dua[k] + SIGMA_STEP * (rel_next[k] - rel[k]), -LAMBDA_BOUND, LAMBDA_BOUND)
        x0_out[rows, :] = img[k] - TAU_STEP * (behind - ahead)
        next_out[rows, :] = rel_next[k]
        zk = small_dot(dg[k], x0_out[rows, :])
        for n in range(NB):
            ys[pl.ds((k * NB + n) * VPAD, VPAD), :] = zk[:, n * BLK : (n + 1) * BLK]
    for v in range(VIEWS):
        hi, lo = split(ys[pl.ds(v, tiles * NB, stride=VPAD), :])
        lhs[v, 0 : tiles * NB, 0:BLK] = hi
        lhs[v, 0 : tiles * NB, BLK : 2 * BLK] = lo
    roll_out(tiles, own_shift)

    sum_rows(group_tables)
    fetch_sino.wait()
    rho[...] = sino[...] - summed()
    pi[...] = jnp.zeros_like(pi)
    gpi[...] = jnp.zeros_like(gpi)
    xi[...] = jnp.zeros_like(xi)

    def inner(a, b):
        return jnp.sum(jnp.sum(a * b, axis=0), keepdims=True)

    def mix_tile(k, _):
        rows = pl.ds(pl.multiple_of(k * NB, NB), NB)
        parts = [mapped[v, rows, :] for v in range(VIEWS)]
        sums = [None] * VIEWS
        row = 0
        for v in range(VIEWS):
            for w in range(v, VIEWS):
                c = mix[k, row : row + 1, :]
                row += 1
                for a, b in ((v, w), (w, v))[: 1 + (v != w)]:
                    term = c * parts[b]
                    sums[a] = term if sums[a] is None else sums[a] + term
        for v in range(VIEWS):
            hi, lo = split(sums[v])
            lhs[v, rows, 0:BLK] = hi
            lhs[v, rows, BLK : 2 * BLK] = lo
        return 0

    def step(it, norm_now):
        roll_back(rho[...], group_tiles, group_shift)
        for v in range(VIEWS):
            mapped[v] = jnp.dot(lhs[v], rt[v], preferred_element_type=F32)
        lax.fori_loop(0, group_tiles, mix_tile, 0)
        roll_out(group_tiles, group_shift)
        sum_group()
        g = summed()
        norm_next = inner(rho[...], g)
        beta = jnp.where(it == 0, 0.0, norm_next / norm_now)
        pi[...] = rho[...] + beta[None] * pi[...]
        gpi[...] = g + beta[None] * gpi[...]
        product = inner(gpi[...], gpi[...]) + inner(pi[...], gpi[...]) / TAU_STEP
        alpha = (norm_next / product)[None]
        xi[...] = xi[...] + alpha * pi[...]
        rho[...] = rho[...] - alpha * (gpi[...] + pi[...] / TAU_STEP)
        return norm_next

    lax.fori_loop(0, CG_ITERS, step, jnp.ones((1, 1), F32))

    roll_back(xi[...], tiles, own_shift)
    for v in range(VIEWS):
        ys[pl.ds(v, tiles * NB, stride=VPAD), :] = jnp.dot(
            lhs[v, 0 : tiles * NB, :], rt[v], preferred_element_type=F32
        )
    for k in range(tiles):
        yk = jnp.concatenate([ys[pl.ds((k * NB + n) * VPAD, VPAD), :] for n in range(NB)], axis=1)
        step_out[pl.ds(k * TR, TR), :] = small_dot(jnp.transpose(dg[k]), yk)
    for c in rel_copies + s_copies:
        c.wait_send()


def local(image, relaxed, dual, sinogram, angle_index, bin_offset, row_weight, response, row_gain):
    rows = image.shape[2]
    tiles = rows // TR
    group_tiles = tiles * NR // GROUP
    block = (tiles, TR, COLS)
    sino = (VIEWS, NB, BLK)
    any_ = pl.BlockSpec(memory_space=pl.ANY)
    vmem = pl.BlockSpec(memory_space=pltpu.VMEM)
    smem = pl.BlockSpec(memory_space=pltpu.SMEM)
    dma = pltpu.SemaphoreType.DMA
    x0, step, ahead = pl.pallas_call(
        solve_kernel,
        name="solve",
        out_shape=(pltpu.VMEM((rows, COLS), F32),) * 3,
        in_specs=[smem, smem, any_, any_, any_, any_, vmem, any_, vmem, vmem],
        out_specs=(vmem,) * 3,
        scratch_shapes=[pltpu.VMEM(block, F32)] * 6
        + [
            pltpu.VMEM(response.shape, BF16),
            pltpu.VMEM(sino, F32),
            pltpu.VMEM(row_weight.shape, F32),
            pltpu.VMEM((VPAD, TR), F32),
            pltpu.VMEM((PAIRS, TR), F32),
            pltpu.VMEM((tiles, VPAD, TR), F32),
            pltpu.VMEM((VIEWS, 2 * BLK, BLK), BF16),
            pltpu.VMEM((VIEWS, 2 * BLK, BLK), BF16),
            pltpu.VMEM((VIEWS, 2 * NB, BLK), F32),
            pltpu.VMEM((VIEWS, group_tiles * NB, 2 * BLK), BF16),
            pltpu.VMEM((VIEWS, group_tiles * NB, BLK), F32),
            pltpu.VMEM((group_tiles, PAIRS, BLK), F32),
            pltpu.VMEM((tiles * NB * VPAD, BLK), F32),
            pltpu.VMEM((HALVES, 8, BLK), F32),
            pltpu.VMEM((HALVES, 8, BLK), F32),
            pltpu.VMEM((NR - 1, 8, BLK), F32),
            pltpu.VMEM((GROUP, CHUNKS, 8, BLK), F32),
        ]
        + [pltpu.VMEM(sino, F32)] * 4
        + [
            pltpu.VMEM((8, BLK), jnp.int32),
            pltpu.VMEM((GROUP_ROWS, 8, BLK), jnp.int32),
            pltpu.VMEM((8, BLK), F32),
            pltpu.VMEM((GROUP_ROWS, 8, BLK), F32),
            pltpu.SMEM((GROUP_ROWS, 8, BLK), jnp.int32),
            pltpu.SMEM((group_tiles * VIEWS,), jnp.int32),
            pltpu.SMEM((group_tiles * VIEWS,), jnp.int32),
        ]
        + [dma((3, tiles)), dma((3,)), pltpu.SemaphoreType.REGULAR((ROUNDS,))]
        + [dma((tiles,))] * 4
        + [dma((2, NR // GROUP)), dma((2, GROUP_ROWS))]
        + [dma(())] * 4
        + [dma((GROUP,))] * 4
        + [pltpu.VMEM((group_tiles, 2 * NB, BLK), F32)] * VIEWS,
        compiler_params=pltpu.CompilerParams(
            collective_id=0, has_side_effects=True, vmem_limit_bytes=VMEM_LIMIT
        ),
    )(
        angle_index,
        bin_offset,
        image.reshape(rows, COLS),
        relaxed.reshape(rows, COLS),
        dual.reshape(rows, COLS),
        sinogram.reshape(sino),
        jnp.transpose(row_weight),
        response,
        row_gain.reshape(1, rows),
        bin_offset,
    )
    image_new = (x0 + step).reshape(image.shape)
    ahead = ahead.reshape(image.shape)
    dual_new = jnp.clip(dual + SIGMA_STEP * (ahead - relaxed), -LAMBDA_BOUND, LAMBDA_BOUND)
    return image_new, dual_new


def solution(mesh):
    return jax.shard_map(
        local,
        mesh=mesh,
        in_specs=(
            P("tm", None, "row", None),
            P("tm", None, "row", None),
            P("tm", None, "row", None),
            P("tm", None, None, None),
            P("tm", None),
            P("row", None),
            P(),
            P(),
            P("row"),
        ),
        out_specs=(P("tm", None, "row", None), P("tm", None, "row", None)),
        check_vma=False,
    )
```

time: 1170 us -> 68.8 us (0.06); the launches traced: 1150 us -> 68 us
  local copies, waits for them, and re-layouts: 910 us -> 0.53 us
  blocking collectives: 89.4 us -> 0 us
  Pallas kernels: 0 us -> 65.1 us
  waiting for transfers between devices: 58.8 us -> 0 us
  other arithmetic: 29 us -> 1.73 us
  matrix products: 22.6 us -> 0 us
  starting transfers between devices: 21.6 us -> 0 us
    gather x1016 -> x0, local copies, waits for them, and re-layouts: 891 us -> none
    all_to_all x6 -> x0, blocking collectives: 89.4 us -> none  [the longest x4 62.9 us: sent_and_summed(): lax.all_to_all(blocks, axis, split_axis=0, concat_axis=0, tiled=True)]
    pallas_call x0 -> x1, Pallas kernels: none -> 65.1 us  [local(): pl.pallas_call(solve_kernel, name='solve', out_shape=(pltpu.VMEM((rows, C...]
    all_to_all x5 -> x0, waiting for transfers between devices: 49.6 us -> none  [copy_for_each(): return lax.all_to_all(copies, axis, split_axis=0, concat_axis=0, tiled=True)]
    dot_general x16 -> x0, matrix products: 22.6 us -> none  [the longest x3 7.59 us: backproject(): tiled = jnp.einsum('vj,vksc->skjc', weights, mapped, precision=HIGH)]
    all_to_all x5 -> x0, starting transfers between devices: 19.9 us -> none  [copy_for_each(): return lax.all_to_all(copies, axis, split_axis=0, concat_axis=0, tiled=True)]
    reduce_sum x18 -> x0, other arithmetic: 12.6 us -> none  [the longest x3 6.5 us: measure(): total, squared = together((partial_value, jnp.sum(volume * volume)), 'row')]
  transfers between devices with their start and end apart: 8 -> 0, of which waited for: 6 -> 0; matrix products, arithmetic and copies ran while one was open for 0% -> 0% of each run, Pallas kernels for 0% -> 0%
where the time goes in v1:
time: 68.8 us; the launch traced here: 68 us
  Pallas kernels  65.1 us (95%)
  other arithmetic  1.73 us (3%)
    pallas_call x1, Pallas kernels, local(): pl.pallas_call(solve_kernel, name='solve', out_shape=(pltpu.VMEM((rows, C...  65.1 us

profile of v1, /device:TPU:2, one launch (start us, length us, event | category | flops | bytes accessed | tf_op | source)
XLA Modules:
  0.0 68.0 jit_solution(15747513891359291597)
XLA Ops:
  0.6 65.1 %solve.1 = (f32[64,2048]{1,0:T(8,128)S(1)}, f32[64,2048]{1,0:T(8,128)S(1)}, f32[64,2048]{1,0:T(8,128)S(1)}) custom-call(s32[1,12]{1,0:T(1,128)} %angles.1, s32[4,32]{1,0:T(4,128)} %offsets_v.1, f32[64,2048]{1,0:T(8,128)} %bitcast.18, f32[64,2048]{1,0:T(8,128)} %bitcast.16, f32[64,2048]{1,0:T(8,128)} %bitcast.17, f32[12,16,128]{2,1,0:T(8,128)} %bitcast.19, ...), custom_call_target="tpu_custom_call" | custom-call | tf_op jit(solution)/shard_map/solve/pallas_call | solution.py:432
  65.8 0.0 copy-start
  65.8 0.0 copy-start.1
  65.8 0.9 %add_bitcast_fusion = f32[1,1,64,2048]{3,2,1,0:T(8,128)} fusion(f32[64,2048]{1,0:T(8,128)S(1)} %get-tuple-element.5, f32[64,2048]{1,0:T(8,128)S(1)} %get-tuple-element.6), kind=kLoop, calls=%fused_computation.4 | loop fusion | flops 131072 | bytes 1572864 | tf_op jit(solution)/shard_map/reshape | solution.py:489
  66.6 0.3 copy-done
  67.0 0.2 copy-done.1
  67.2 0.9 %fusion.2 = f32[1,1,64,2048]{3,2,1,0:T(8,128)} fusion(f32[1,1,64,2048]{3,2,1,0:T(8,128)S(1)} %copy-done.1, f32[1,1,64,2048]{3,2,1,0:T(8,128)S(1)} %copy-done, f32[64,2048]{1,0:T(8,128)S(1)} %get-tuple-element.7), kind=kLoop, calls=%fused_computation.3 | loop fusion | flops 524288 | bytes 2097152 | tf_op jit(solution)/shard_map/jit(clip)/min | solution.py:491
Async XLA Ops:
  65.8 1.2 %copy-start = (f32[1,1,64,2048]{3,2,1,0:T(8,128)S(1)}, f32[1,1,64,2048]{3,2,1,0:T(8,128)}, u32[]{:S(2)}) copy-start(f32[1,1,64,2048]{3,2,1,0:T(8,128)} %param.10) | copy-start | bytes 1572868
  65.8 1.4 %copy-start.1 = (f32[1,1,64,2048]{3,2,1,0:T(8,128)S(1)}, f32[1,1,64,2048]{3,2,1,0:T(8,128)}, u32[]{:S(2)}) copy-start(f32[1,1,64,2048]{3,2,1,0:T(8,128)} %param.11) | copy-start | bytes 1572868
